TPU v7x, 32 devices: a whole 2x2x4 slice. The times are simulated.
32 devices in a mesh: row: 4 (over y, x), col: 8 (over z, core).
Axes of the slice: x: 2, y: 2, z: 4, core: 2. Of those that a mesh axis runs over, the one named last changes fastest.
Arguments:
- features: bfloat16 [8192, 512], P(('row', 'col')), may hold values from -6 to 6
- tile_values: bfloat16 [4, 8, 128, 128, 128], P('row', 'col'), may hold values from -0.1875 to 0.1875
- tile_places: int32 [4, 8, 2, 128], P('row', 'col'), may hold values from 0 to 15, as said below
- tile_counts: int32 [4, 8], replicated, may hold values from 40 to 128, as said below
- weight_one: float32 [512, 512], replicated, may hold values from -0.25 to 0.25
- weight_two: float32 [512, 512], replicated, may hold values from -0.25 to 0.25
Outputs:
- embedded: float32 [8192, 512], P(('row', 'col'))
Inputs may be any that keep to these rules, and one draw needn't show every extreme that they name: `tile_places`: in every block the first tile_counts slots name distinct tiles with tile rows below 16 and tile columns below 8, listed in order of tile row (never falling); later slots also name tiles in range. `tile_counts`: some block has exactly 128 tiles.
All inputs are finite; a program needn't handle non-finite values.
Results may differ from a plain program's by a relative error of at most 0.0029.
Values may be sent and summed in bfloat16 or wider, within the bound.
A program may use at most 64 MiB of HBM per device.

v0:
```python
import jax
import jax.numpy as jnp
from jax import lax
from jax.sharding import PartitionSpec as P

TR = 16


def add_slots(
    partial_value, blocks, row_ids, col_ids, column_tiles, first_slot, stop_slot, row_base
):
    slot_count = blocks.shape[0]
    group_size = min(16, slot_count)
    last_row = partial_value.shape[0] - 1

    def one_turn(group, totals):
        offset = jnp.minimum(group * group_size, slot_count - group_size)
        tile_group = lax.dynamic_slice_in_dim(blocks, offset, group_size, 0)
        group_rows = lax.dynamic_slice_in_dim(row_ids, offset, group_size, 0)
        group_cols = lax.dynamic_slice_in_dim(col_ids, offset, group_size, 0)
        positions = offset + jnp.arange(group_size, dtype=jnp.int32)
        active = (positions >= jnp.maximum(first_slot, group * group_size)) & (
            positions < stop_slot
        )
        products = jnp.einsum(
            "sij,sjf->sif", tile_group, column_tiles[group_cols], preferred_element_type=jnp.float32
        )
        products = jnp.where(active[:, None, None], products, 0.0)
        local_rows = jnp.clip(group_rows - row_base, 0, last_row)
        return totals.at[local_rows].add(products)

    first_turn = first_slot // group_size
    last_turn = (stop_slot + group_size - 1) // group_size
    return lax.fori_loop(first_turn, last_turn, one_turn, partial_value)


def shards(features, tile_values, tile_places, tile_counts, weight_one, weight_two):
    blocks = tile_values.reshape(tile_values.shape[2:])
    places = tile_places.reshape(tile_places.shape[2:])
    tile_size = blocks.shape[1]
    width_all = features.shape[1]
    block_row = lax.axis_index("row")
    block_col = lax.axis_index("col")
    own_count = tile_counts[block_row, block_col]

    def layer(inputs, weights):
        gathered = lax.all_gather(inputs, "row", axis=0, tiled=True)
        column_tiles = gathered.reshape(gathered.shape[0] // tile_size, tile_size, width_all)
        partial_value = jnp.zeros((TR, tile_size, width_all), jnp.float32)
        partial_value = add_slots(
            partial_value, blocks, places[0], places[1], column_tiles, 0, own_count, 0
        )
        mine = lax.psum_scatter(
            partial_value.reshape(TR * tile_size, width_all), "col", scatter_dimension=0, tiled=True
        )
        return jnp.maximum(jnp.dot(mine, weights, precision=lax.Precision.HIGHEST), 0.0)

    hidden = layer(features, weight_one).astype(jnp.bfloat16)
    return layer(hidden, weight_two)


def solution(mesh):
    placed = (
        P(("row", "col"), None),
        P("row", "col", None, None, None),
        P("row", "col", None, None),
        P(),
        P(),
        P(),
    )
    return jax.shard_map(
        shards, mesh=mesh, in_specs=placed, out_specs=P(("row", "col"), None), check_vma=False
    )
```

profile of v0, /device:TPU:0, one launch (start us, length us, event | category | flops | bytes accessed | tf_op | source)
XLA Modules:
  0.0 428.9 jit_solution(628005692319676586)
XLA Ops:
  7.3 1.3 dynamic_slice.21
  9.4 0.8 slice_bitcast_fusion
  10.1 28.3 %all-gather.3.cloned.1.call-done = bf16[1024,512]{1,0:T(8,128)(2,1)} async-done(((bf16[256,512]{1,0:T(8,128)(2,1)}), bf16[1024,512]{1,0:T(8,128)(2,1)}) %all-gather.3.cloned.1.call-update) | async-done | bytes 1048592 | tf_op jit(solution)/shard_map/all_gather | solution.py:47
  38.4 2.5 broadcast.45.clone
  41.0 91.4 %while.20 = (s32[]{:T(128)}, f32[16,128,512]{2,1,0:T(8,128)}, s32[]{:T(128)}, s32[128]{0:T(128)S(1)}, s32[]{:T(128)}, /*index=5*/bf16[128,128,128]{2,1,0:T(8,128...) while((s32[]{:T(128)}, f32[16,128,512]{2,1,0:T(8,128)}, ...), condition=%wide.region_2.3_spmd, body=%wide.region_0.2_spmd.sunk | while | flops 270533824 | bytes 23597752 | solution.py:34
  41.0 1.9 gather_fusion
  43.7 3.7 convolution_select_fusion.4
  47.3 8.8 %scatter_fusion = f32[16,128,512]{2,1,0:T(8,128)} fusion(f32[16,128,512]{2,1,0:T(8,128)} %get-tuple-element.253, s32[16]{0:T(128)S(1)} %get-tuple-element.227, f32[16,128,512]{2,1,0:T(8,128)} %convolution_select_fusion.4), kind=kCustom, calls=%fused_computation.2.clone.1 | custom fusion | flops 1048576 | bytes 12582976 | tf_op jit(solution)/shard_map/while/body/scatter-add | solution.py:30
  56.2 1.9 gather_fusion
  58.9 3.7 convolution_select_fusion.4
  62.5 8.8 %scatter_fusion = f32[16,128,512]{2,1,0:T(8,128)} fusion(f32[16,128,512]{2,1,0:T(8,128)} %get-tuple-element.253, s32[16]{0:T(128)S(1)} %get-tuple-element.227, f32[16,128,512]{2,1,0:T(8,128)} %convolution_select_fusion.4), kind=kCustom, calls=%fused_computation.2.clone.1 | custom fusion | flops 1048576 | bytes 12582976 | tf_op jit(solution)/shard_map/while/body/scatter-add | solution.py:30
  71.4 1.9 gather_fusion
  74.1 3.7 convolution_select_fusion.4
  77.7 8.7 %scatter_fusion = f32[16,128,512]{2,1,0:T(8,128)} fusion(f32[16,128,512]{2,1,0:T(8,128)} %get-tuple-element.253, s32[16]{0:T(128)S(1)} %get-tuple-element.227, f32[16,128,512]{2,1,0:T(8,128)} %convolution_select_fusion.4), kind=kCustom, calls=%fused_computation.2.clone.1 | custom fusion | flops 1048576 | bytes 12582976 | tf_op jit(solution)/shard_map/while/body/scatter-add | solution.py:30
  86.5 1.9 gather_fusion
  89.1 3.7 convolution_select_fusion.4
  92.8 8.9 %scatter_fusion = f32[16,128,512]{2,1,0:T(8,128)} fusion(f32[16,128,512]{2,1,0:T(8,128)} %get-tuple-element.253, s32[16]{0:T(128)S(1)} %get-tuple-element.227, f32[16,128,512]{2,1,0:T(8,128)} %convolution_select_fusion.4), kind=kCustom, calls=%fused_computation.2.clone.1 | custom fusion | flops 1048576 | bytes 12582976 | tf_op jit(solution)/shard_map/while/body/scatter-add | solution.py:30
  101.8 1.9 gather_fusion
  104.4 3.7 convolution_select_fusion.4
  108.1 8.9 %scatter_fusion = f32[16,128,512]{2,1,0:T(8,128)} fusion(f32[16,128,512]{2,1,0:T(8,128)} %get-tuple-element.253, s32[16]{0:T(128)S(1)} %get-tuple-element.227, f32[16,128,512]{2,1,0:T(8,128)} %convolution_select_fusion.4), kind=kCustom, calls=%fused_computation.2.clone.1 | custom fusion | flops 1048576 | bytes 12582976 | tf_op jit(solution)/shard_map/while/body/scatter-add | solution.py:30
  117.1 1.9 gather_fusion
  119.7 3.7 convolution_select_fusion.4
  123.4 9.0 %scatter_fusion = f32[16,128,512]{2,1,0:T(8,128)} fusion(f32[16,128,512]{2,1,0:T(8,128)} %get-tuple-element.253, s32[16]{0:T(128)S(1)} %get-tuple-element.227, f32[16,128,512]{2,1,0:T(8,128)} %convolution_select_fusion.4), kind=kCustom, calls=%fused_computation.2.clone.1 | custom fusion | flops 1048576 | bytes 12582976 | tf_op jit(solution)/shard_map/while/body/scatter-add | solution.py:30
  132.5 82.7 %reduce-scatter.3.cloned.1.call-done = f32[256,512]{1,0:T(8,128)} async-done(((f32[2048,512]{1,0:T(8,128)}), f32[256,512]{1,0:T(8,128)}) %reduce-scatter.3.cloned.1.call-update) | async-done | bytes 524304 | tf_op jit(solution)/shard_map/reduce_scatter | solution.py:53
  215.2 2.8 fusion.4
  218.1 25.1 %all-gather.5.cloned.1.call-done = bf16[1024,512]{1,0:T(8,128)(2,1)} async-done(((bf16[256,512]{1,0:T(8,128)(2,1)}), bf16[1024,512]{1,0:T(8,128)(2,1)}) %all-gather.5.cloned.1.call-update) | async-done | bytes 1048592 | tf_op jit(solution)/shard_map/all_gather | solution.py:47
  243.1 2.5 broadcast.45
  245.6 91.7 %while.21 = (s32[]{:T(128)}, f32[16,128,512]{2,1,0:T(8,128)}, s32[]{:T(128)}, s32[128]{0:T(128)S(1)}, s32[]{:T(128)}, /*index=5*/bf16[128,128,128]{2,1,0:T(8,128...) while((s32[]{:T(128)}, f32[16,128,512]{2,1,0:T(8,128)}, ...), condition=%wide.region_6.7_spmd, body=%wide.region_4.6_spmd.sunk | while | flops 270533824 | bytes 23597752 | solution.py:34
  245.7 1.9 gather_fusion.1
  248.3 3.7 convolution_select_fusion.5
  252.0 9.1 %scatter_fusion.1 = f32[16,128,512]{2,1,0:T(8,128)} fusion(f32[16,128,512]{2,1,0:T(8,128)} %get-tuple-element.292, s32[16]{0:T(128)S(1)} %get-tuple-element.237, f32[16,128,512]{2,1,0:T(8,128)} %convolution_select_fusion.5), kind=kCustom, calls=%fused_computation.3.clone.1 | custom fusion | flops 1048576 | bytes 12582976 | tf_op jit(solution)/shard_map/while/body/scatter-add | solution.py:30
  261.2 1.9 gather_fusion.1
  263.8 3.7 convolution_select_fusion.5
  267.5 8.8 %scatter_fusion.1 = f32[16,128,512]{2,1,0:T(8,128)} fusion(f32[16,128,512]{2,1,0:T(8,128)} %get-tuple-element.292, s32[16]{0:T(128)S(1)} %get-tuple-element.237, f32[16,128,512]{2,1,0:T(8,128)} %convolution_select_fusion.5), kind=kCustom, calls=%fused_computation.3.clone.1 | custom fusion | flops 1048576 | bytes 12582976 | tf_op jit(solution)/shard_map/while/body/scatter-add | solution.py:30
  276.4 1.9 gather_fusion.1
  279.0 3.7 convolution_select_fusion.5
  282.8 8.8 %scatter_fusion.1 = f32[16,128,512]{2,1,0:T(8,128)} fusion(f32[16,128,512]{2,1,0:T(8,128)} %get-tuple-element.292, s32[16]{0:T(128)S(1)} %get-tuple-element.237, f32[16,128,512]{2,1,0:T(8,128)} %convolution_select_fusion.5), kind=kCustom, calls=%fused_computation.3.clone.1 | custom fusion | flops 1048576 | bytes 12582976 | tf_op jit(solution)/shard_map/while/body/scatter-add | solution.py:30
  291.7 1.9 gather_fusion.1
  294.3 3.7 convolution_select_fusion.5
  298.0 8.8 %scatter_fusion.1 = f32[16,128,512]{2,1,0:T(8,128)} fusion(f32[16,128,512]{2,1,0:T(8,128)} %get-tuple-element.292, s32[16]{0:T(128)S(1)} %get-tuple-element.237, f32[16,128,512]{2,1,0:T(8,128)} %convolution_select_fusion.5), kind=kCustom, calls=%fused_computation.3.clone.1 | custom fusion | flops 1048576 | bytes 12582976 | tf_op jit(solution)/shard_map/while/body/scatter-add | solution.py:30
  306.9 1.9 gather_fusion.1
  309.5 3.7 convolution_select_fusion.5
  313.2 8.8 %scatter_fusion.1 = f32[16,128,512]{2,1,0:T(8,128)} fusion(f32[16,128,512]{2,1,0:T(8,128)} %get-tuple-element.292, s32[16]{0:T(128)S(1)} %get-tuple-element.237, f32[16,128,512]{2,1,0:T(8,128)} %convolution_select_fusion.5), kind=kCustom, calls=%fused_computation.3.clone.1 | custom fusion | flops 1048576 | bytes 12582976 | tf_op jit(solution)/shard_map/while/body/scatter-add | solution.py:30
  322.1 1.9 gather_fusion.1
  324.7 3.7 convolution_select_fusion.5
  328.5 8.8 %scatter_fusion.1 = f32[16,128,512]{2,1,0:T(8,128)} fusion(f32[16,128,512]{2,1,0:T(8,128)} %get-tuple-element.292, s32[16]{0:T(128)S(1)} %get-tuple-element.237, f32[16,128,512]{2,1,0:T(8,128)} %convolution_select_fusion.5), kind=kCustom, calls=%fused_computation.3.clone.1 | custom fusion | flops 1048576 | bytes 12582976 | tf_op jit(solution)/shard_map/while/body/scatter-add | solution.py:30
  337.3 82.1 %reduce-scatter.5.cloned.1.call-done = f32[256,512]{1,0:T(8,128)} async-done(((f32[2048,512]{1,0:T(8,128)}), f32[256,512]{1,0:T(8,128)}) %reduce-scatter.5.cloned.1.call-update) | async-done | bytes 524304 | tf_op jit(solution)/shard_map/reduce_scatter | solution.py:53
  419.5 2.9 convolution_maximum_fusion
  (48 shorter events, 10.2 us)
Async XLA Ops:
  6.5 208.6 %copy-start = (f32[512,512]{1,0:T(8,128)S(1)}, f32[512,512]{1,0:T(8,128)}, u32[]{:S(2)}) copy-start(f32[512,512]{1,0:T(8,128)} %param.14) | copy-start | bytes 3145732
  6.5 31.9 %all-gather.3.cloned.1.call-start = ((), (), s32[]{:S(2)}) async-start(), calls=%async_computation.2 | async-start | bytes 1310720 | tf_op jit(solution)/shard_map/all_gather | solution.py:47
  7.3 207.9 %reduce-scatter.3.cloned.1.call-start = ((), (), s32[]{:S(2)}) async-start(), calls=%async_computation.3 | async-start | bytes 4718592 | tf_op jit(solution)/shard_map/reduce_scatter | solution.py:53
  132.4 110.7 %all-gather.5.cloned.1.call-start = ((), (), s32[]{:S(2)}) async-start(), calls=%async_computation.4 | async-start | bytes 1310720 | tf_op jit(solution)/shard_map/all_gather | solution.py:47
  218.0 201.5 %reduce-scatter.5.cloned.1.call-start = ((), (), s32[]{:S(2)}) async-start(), calls=%async_computation.5 | async-start | bytes 4718592 | tf_op jit(solution)/shard_map/reduce_scatter | solution.py:53
  337.3 82.2 %copy-start.1 = (f32[512,512]{1,0:T(8,128)S(1)}, f32[512,512]{1,0:T(8,128)}, u32[]{:S(2)}) copy-start(f32[512,512]{1,0:T(8,128)} %param.15) | copy-start | bytes 3145732
Sparse Core Ops, SparseCore 0:
  9.2 29.2 all-gather.2
  132.5 82.5 reduce-scatter.2
  218.1 24.9 all-gather.4
  337.4 81.9 reduce-scatter.4
where the time goes:
time: 431 us; the launch traced here: 429 us
  waiting for transfers between devices  219 us (51%)
  other arithmetic  116 us (27%)
  matrix products  50.2 us (12%)
  local copies, waits for them, and re-layouts  30 us (7%)
  between operations  13.9 us (3%)
    reduce_scatter x2, waiting for transfers between devices, layer(): lax.psum_scatter(partial_value.reshape(TR * tile_size, width_all), 'col',...  165 us
    scatter-add x12, other arithmetic, one_turn(): return totals.at[local_rows].add(products)  106 us
    all_gather x2, waiting for transfers between devices, layer(): gathered = lax.all_gather(inputs, 'row', axis=0, tiled=True)  53.4 us
    dot_general x12, matrix products, one_turn(): jnp.einsum('sij,sjf->sif', tile_group, column_tiles[group_cols], preferre...  44.5 us
    gather x12, local copies, waits for them, and re-layouts, one_turn(): column_tiles[group_cols]  22.9 us
  transfers between devices with their start and end apart: 4, of which 4 were waited for; matrix products, arithmetic and copies ran while one was open for 0% of the time, Pallas kernels for 0%

commit v1 on v0

--- a/solution.py
+++ b/solution.py
@@ -44,7 +44,14 @@
     own_count = tile_counts[block_row, block_col]
 
     def layer(inputs, weights):
-        gathered = lax.all_gather(inputs, "row", axis=0, tiled=True)
+        ring = [inputs]
+        for hop in range(3):
+            ring.append(lax.ppermute(ring[-1], "row", [(dev, (dev + 1) % 4) for dev in range(4)]))
+        gathered = jnp.roll(
+            jnp.concatenate(ring[::-1], axis=0),
+            (lax.axis_index("row") + 1) * ring[0].shape[0],
+            axis=0,
+        )
         column_tiles = gathered.reshape(gathered.shape[0] // tile_size, tile_size, width_all)
         partial_value = jnp.zeros((TR, tile_size, width_all), jnp.float32)
         partial_value = add_slots(

time: 431 us -> 436 us (1.012)
  waiting for transfers between devices: 219 us -> 204 us
  other arithmetic: 116 us -> 129 us
  starting transfers between devices: 0.12 us -> 7.51 us
    all_gather x2 -> x0, waiting for transfers between devices: 53.4 us -> none  [layer(): gathered = lax.all_gather(inputs, 'row', axis=0, tiled=True)]
    ppermute x0 -> x6, waiting for transfers between devices: none -> 38.7 us  [layer(): lax.ppermute(ring[-1], 'row', [(dev, (dev + 1) % 4) for dev in range(4)])]
    concatenate x0 -> x2, other arithmetic: none -> 13.6 us  [layer(): jnp.roll(jnp.concatenate(ring[::-1], axis=0), (lax.axis_index('row') + 1)...]
    ppermute x0 -> x6, starting transfers between devices: none -> 7.47 us  [layer(): lax.ppermute(ring[-1], 'row', [(dev, (dev + 1) % 4) for dev in range(4)])]
  transfers between devices with their start and end apart: 4 -> 8, of which waited for: 4 -> 8; matrix products, arithmetic and copies ran while one was open for 0% -> 0% of each run, Pallas kernels for 0% -> 0%
where the time goes in v1:
time: 436 us; the launch traced here: 434 us
  waiting for transfers between devices  204 us (47%)
  other arithmetic  129 us (30%)
  matrix products  49.2 us (11%)
  local copies, waits for them, and re-layouts  30 us (7%)
  between operations  14.1 us (3%)
  starting transfers between devices  7.51 us (2%)
    reduce_scatter x2, waiting for transfers between devices, layer(): lax.psum_scatter(partial_value.reshape(TR * tile_size, width_all), 'col',...  165 us
    scatter-add x12, other arithmetic, one_turn(): return totals.at[local_rows].add(products)  106 us
    dot_general x12, matrix products, one_turn(): jnp.einsum('sij,sjf->sif', tile_group, column_tiles[group_cols], preferre...  44.2 us
    ppermute x6, waiting for transfers between devices, layer(): lax.ppermute(ring[-1], 'row', [(dev, (dev + 1) % 4) for dev in range(4)])  38.7 us
    gather x12, local copies, waits for them, and re-layouts, one_turn(): column_tiles[group_cols]  22.9 us
    concatenate x2, other arithmetic, layer(): jnp.roll(jnp.concatenate(ring[::-1], axis=0), (lax.axis_index('row') + 1)...  13.6 us
  transfers between devices with their start and end apart: 8, of which 8 were waited for; matrix products, arithmetic and copies ran while one was open for 0% of the time, Pallas kernels for 0%

profile of v1, /device:TPU:0, one launch (start us, length us, event | category | flops | bytes accessed | tf_op | source)
XLA Modules:
  0.0 433.9 jit_solution(4403239344351083126)
XLA Ops:
  6.5 3.0 collective-permute-start
  9.5 7.5 %collective-permute-done = bf16[256,512]{1,0:T(8,128)(2,1)S(1)} collective-permute-done((bf16[256,512]{1,0:T(8,128)(2,1)}, bf16[256,512]{1,0:T(8,128)(2,1)S(1)}, u32[]{:S(2)}, u32[]{:S(2)}) %collective-permute-start) | collective-permute-done | bytes 262176 | tf_op jit(solution)/shard_map/ppermute | solution.py:49
  17.8 7.6 %collective-permute-done.1 = bf16[256,512]{1,0:T(8,128)(2,1)S(1)} collective-permute-done((bf16[256,512]{1,0:T(8,128)(2,1)S(1)}, bf16[256,512]{1,0:T(8,128)(2,1)S(1)}, u32[]{:S(2)}, u32[]{:S(2)}) %collective-permute-start.1) | collective-permute-done | bytes 262176 | tf_op jit(solution)/shard_map/ppermute | solution.py:49
  28.2 4.7 %collective-permute-done.2 = bf16[256,512]{1,0:T(8,128)(2,1)S(1)} collective-permute-done((bf16[256,512]{1,0:T(8,128)(2,1)S(1)}, bf16[256,512]{1,0:T(8,128)(2,1)S(1)}, u32[]{:S(2)}, u32[]{:S(2)}) %collective-permute-start.2) | collective-permute-done | bytes 262176 | tf_op jit(solution)/shard_map/ppermute | solution.py:49
  32.9 6.7 %fusion.15 = bf16[1024,512]{1,0:T(8,128)(2,1)} fusion(s32[]{:T(128)S(6)} %select_n.56, bf16[256,512]{1,0:T(8,128)(2,1)S(1)} %collective-permute-done.2, bf16[256,512]{1,0:T(8,128)(2,1)S(1)} %collective-permute-done.1, bf16[256,512]{1,0:T(8,128)(2,1)S(1)} %collective-permute-done, bf16[256,512]{1,0:T(8,128)(2,1)} %param.12), kind=kLoop, calls=%fused_computation.47 | loop fusion | flops 8388608 | bytes 2097156 | tf_op jit(solution)/shard_map/jit(_roll_dynamic)/concatenate | solution.py:50
  39.6 2.5 broadcast.46.clone
  42.1 91.4 %while.20 = (s32[]{:T(128)}, f32[16,128,512]{2,1,0:T(8,128)}, s32[]{:T(128)}, s32[128]{0:T(128)S(1)}, s32[]{:T(128)}, /*index=5*/bf16[128,128,128]{2,1,0:T(8,128...) while((s32[]{:T(128)}, f32[16,128,512]{2,1,0:T(8,128)}, ...), condition=%wide.region_2.4_spmd, body=%wide.region_0.3_spmd.sunk | while | flops 270533824 | bytes 23597752 | solution.py:34
  42.2 1.9 gather_fusion
  44.8 3.7 convolution_select_fusion.4
  48.5 8.8 %scatter_fusion = f32[16,128,512]{2,1,0:T(8,128)} fusion(f32[16,128,512]{2,1,0:T(8,128)} %get-tuple-element.254, s32[16]{0:T(128)S(1)} %get-tuple-element.228, f32[16,128,512]{2,1,0:T(8,128)} %convolution_select_fusion.4), kind=kCustom, calls=%fused_computation.2.clone.1 | custom fusion | flops 1048576 | bytes 12582976 | tf_op jit(solution)/shard_map/while/body/scatter-add | solution.py:30
  57.4 1.9 gather_fusion
  60.0 3.7 convolution_select_fusion.4
  63.7 8.8 %scatter_fusion = f32[16,128,512]{2,1,0:T(8,128)} fusion(f32[16,128,512]{2,1,0:T(8,128)} %get-tuple-element.254, s32[16]{0:T(128)S(1)} %get-tuple-element.228, f32[16,128,512]{2,1,0:T(8,128)} %convolution_select_fusion.4), kind=kCustom, calls=%fused_computation.2.clone.1 | custom fusion | flops 1048576 | bytes 12582976 | tf_op jit(solution)/shard_map/while/body/scatter-add | solution.py:30
  72.6 1.9 gather_fusion
  75.2 3.7 convolution_select_fusion.4
  78.9 8.7 %scatter_fusion = f32[16,128,512]{2,1,0:T(8,128)} fusion(f32[16,128,512]{2,1,0:T(8,128)} %get-tuple-element.254, s32[16]{0:T(128)S(1)} %get-tuple-element.228, f32[16,128,512]{2,1,0:T(8,128)} %convolution_select_fusion.4), kind=kCustom, calls=%fused_computation.2.clone.1 | custom fusion | flops 1048576 | bytes 12582976 | tf_op jit(solution)/shard_map/while/body/scatter-add | solution.py:30
  87.7 1.9 gather_fusion
  90.3 3.7 convolution_select_fusion.4
  94.0 8.9 %scatter_fusion = f32[16,128,512]{2,1,0:T(8,128)} fusion(f32[16,128,512]{2,1,0:T(8,128)} %get-tuple-element.254, s32[16]{0:T(128)S(1)} %get-tuple-element.228, f32[16,128,512]{2,1,0:T(8,128)} %convolution_select_fusion.4), kind=kCustom, calls=%fused_computation.2.clone.1 | custom fusion | flops 1048576 | bytes 12582976 | tf_op jit(solution)/shard_map/while/body/scatter-add | solution.py:30
  105.6 3.7 convolution_select_fusion.4
  109.2 8.9 %scatter_fusion = f32[16,128,512]{2,1,0:T(8,128)} fusion(f32[16,128,512]{2,1,0:T(8,128)} %get-tuple-element.254, s32[16]{0:T(128)S(1)} %get-tuple-element.228, f32[16,128,512]{2,1,0:T(8,128)} %convolution_select_fusion.4), kind=kCustom, calls=%fused_computation.2.clone.1 | custom fusion | flops 1048576 | bytes 12582976 | tf_op jit(solution)/shard_map/while/body/scatter-add | solution.py:30
  120.8 3.7 convolution_select_fusion.4
  124.5 9.0 %scatter_fusion = f32[16,128,512]{2,1,0:T(8,128)} fusion(f32[16,128,512]{2,1,0:T(8,128)} %get-tuple-element.254, s32[16]{0:T(128)S(1)} %get-tuple-element.228, f32[16,128,512]{2,1,0:T(8,128)} %convolution_select_fusion.4), kind=kCustom, calls=%fused_computation.2.clone.1 | custom fusion | flops 1048576 | bytes 12582976 | tf_op jit(solution)/shard_map/while/body/scatter-add | solution.py:30
  133.6 81.5 %reduce-scatter.3.cloned.1.call-done = f32[256,512]{1,0:T(8,128)} async-done(((f32[2048,512]{1,0:T(8,128)}), f32[256,512]{1,0:T(8,128)}) %reduce-scatter.3.cloned.1.call-update) | async-done | bytes 524304 | tf_op jit(solution)/shard_map/reduce_scatter | solution.py:60
  215.1 2.1 fusion.4
  218.7 5.8 %collective-permute-done.3 = bf16[256,512]{1,0:T(8,128)(2,1)S(1)} collective-permute-done((bf16[256,512]{1,0:T(8,128)(2,1)S(1)}, bf16[256,512]{1,0:T(8,128)(2,1)S(1)}, u32[]{:S(2)}, u32[]{:S(2)}) %collective-permute-start.3) | collective-permute-done | bytes 262176 | tf_op jit(solution)/shard_map/ppermute | solution.py:49
  225.7 7.0 %collective-permute-done.4 = bf16[256,512]{1,0:T(8,128)(2,1)S(1)} collective-permute-done((bf16[256,512]{1,0:T(8,128)(2,1)S(1)}, bf16[256,512]{1,0:T(8,128)(2,1)S(1)}, u32[]{:S(2)}, u32[]{:S(2)}) %collective-permute-start.4) | collective-permute-done | bytes 262176 | tf_op jit(solution)/shard_map/ppermute | solution.py:49
  233.8 6.2 %collective-permute-done.5 = bf16[256,512]{1,0:T(8,128)(2,1)S(1)} collective-permute-done((bf16[256,512]{1,0:T(8,128)(2,1)S(1)}, bf16[256,512]{1,0:T(8,128)(2,1)S(1)}, u32[]{:S(2)}, u32[]{:S(2)}) %collective-permute-start.5) | collective-permute-done | bytes 262176 | tf_op jit(solution)/shard_map/ppermute | solution.py:49
  239.9 6.9 %fusion.8 = bf16[1024,512]{1,0:T(8,128)(2,1)} fusion(s32[]{:T(128)S(6)} %select_n.56, bf16[256,512]{1,0:T(8,128)(2,1)S(1)} %collective-permute-done.5, bf16[256,512]{1,0:T(8,128)(2,1)S(1)} %collective-permute-done.4, bf16[256,512]{1,0:T(8,128)(2,1)S(1)} %collective-permute-done.3, bf16[256,512]{1,0:T(8,128)(2,1)S(1)} %fusion.4), kind=kLoop, calls=%fused_computation.40 | loop fusion | flops 8388608 | bytes 2097156 | tf_op jit(solution)/shard_map/jit(_roll_dynamic)/concatenate | solution.py:50
  246.8 2.5 broadcast.46
  249.3 91.4 %while.21 = (s32[]{:T(128)}, f32[16,128,512]{2,1,0:T(8,128)}, s32[]{:T(128)}, s32[128]{0:T(128)S(1)}, s32[]{:T(128)}, /*index=5*/bf16[128,128,128]{2,1,0:T(8,128...) while((s32[]{:T(128)}, f32[16,128,512]{2,1,0:T(8,128)}, ...), condition=%wide.region_6.8_spmd, body=%wide.region_4.7_spmd.sunk | while | flops 270533824 | bytes 23597752 | solution.py:34
  249.4 1.9 gather_fusion.1
  252.0 3.7 convolution_select_fusion.5
  255.7 8.8 %scatter_fusion.1 = f32[16,128,512]{2,1,0:T(8,128)} fusion(f32[16,128,512]{2,1,0:T(8,128)} %get-tuple-element.293, s32[16]{0:T(128)S(1)} %get-tuple-element.238, f32[16,128,512]{2,1,0:T(8,128)} %convolution_select_fusion.5), kind=kCustom, calls=%fused_computation.3.clone.1 | custom fusion | flops 1048576 | bytes 12582976 | tf_op jit(solution)/shard_map/while/body/scatter-add | solution.py:30
  267.3 3.7 convolution_select_fusion.5
  270.9 8.8 %scatter_fusion.1 = f32[16,128,512]{2,1,0:T(8,128)} fusion(f32[16,128,512]{2,1,0:T(8,128)} %get-tuple-element.293, s32[16]{0:T(128)S(1)} %get-tuple-element.238, f32[16,128,512]{2,1,0:T(8,128)} %convolution_select_fusion.5), kind=kCustom, calls=%fused_computation.3.clone.1 | custom fusion | flops 1048576 | bytes 12582976 | tf_op jit(solution)/shard_map/while/body/scatter-add | solution.py:30
  282.4 3.7 convolution_select_fusion.5
  286.1 8.7 %scatter_fusion.1 = f32[16,128,512]{2,1,0:T(8,128)} fusion(f32[16,128,512]{2,1,0:T(8,128)} %get-tuple-element.293, s32[16]{0:T(128)S(1)} %get-tuple-element.238, f32[16,128,512]{2,1,0:T(8,128)} %convolution_select_fusion.5), kind=kCustom, calls=%fused_computation.3.clone.1 | custom fusion | flops 1048576 | bytes 12582976 | tf_op jit(solution)/shard_map/while/body/scatter-add | solution.py:30
  294.9 1.9 gather_fusion.1
  297.5 3.7 convolution_select_fusion.5
  301.2 8.9 %scatter_fusion.1 = f32[16,128,512]{2,1,0:T(8,128)} fusion(f32[16,128,512]{2,1,0:T(8,128)} %get-tuple-element.293, s32[16]{0:T(128)S(1)} %get-tuple-element.238, f32[16,128,512]{2,1,0:T(8,128)} %convolution_select_fusion.5), kind=kCustom, calls=%fused_computation.3.clone.1 | custom fusion | flops 1048576 | bytes 12582976 | tf_op jit(solution)/shard_map/while/body/scatter-add | solution.py:30
  312.8 3.7 convolution_select_fusion.5
  316.5 8.9 %scatter_fusion.1 = f32[16,128,512]{2,1,0:T(8,128)} fusion(f32[16,128,512]{2,1,0:T(8,128)} %get-tuple-element.293, s32[16]{0:T(128)S(1)} %get-tuple-element.238, f32[16,128,512]{2,1,0:T(8,128)} %convolution_select_fusion.5), kind=kCustom, calls=%fused_computation.3.clone.1 | custom fusion | flops 1048576 | bytes 12582976 | tf_op jit(solution)/shard_map/while/body/scatter-add | solution.py:30
  325.4 1.9 gather_fusion.1
  328.1 3.7 convolution_select_fusion.5
  331.7 9.0 %scatter_fusion.1 = f32[16,128,512]{2,1,0:T(8,128)} fusion(f32[16,128,512]{2,1,0:T(8,128)} %get-tuple-element.293, s32[16]{0:T(128)S(1)} %get-tuple-element.238, f32[16,128,512]{2,1,0:T(8,128)} %convolution_select_fusion.5), kind=kCustom, calls=%fused_computation.3.clone.1 | custom fusion | flops 1048576 | bytes 12582976 | tf_op jit(solution)/shard_map/while/body/scatter-add | solution.py:30
  340.8 83.4 %reduce-scatter.5.cloned.1.call-done = f32[256,512]{1,0:T(8,128)} async-done(((f32[2048,512]{1,0:T(8,128)}), f32[256,512]{1,0:T(8,128)}) %reduce-scatter.5.cloned.1.call-update) | async-done | bytes 524304 | tf_op jit(solution)/shard_map/reduce_scatter | solution.py:60
  424.2 2.9 convolution_maximum_fusion
  (56 shorter events, 25.6 us)
Async XLA Ops:
  6.5 208.6 %copy-start = (f32[512,512]{1,0:T(8,128)S(1)}, f32[512,512]{1,0:T(8,128)}, u32[]{:S(2)}) copy-start(f32[512,512]{1,0:T(8,128)} %param.16) | copy-start | bytes 3145732
  6.5 208.6 %reduce-scatter.3.cloned.1.call-start = ((), (), s32[]{:S(2)}) async-start(), calls=%async_computation.2 | async-start | bytes 4718592 | tf_op jit(solution)/shard_map/reduce_scatter | solution.py:60
  6.5 10.4 %collective-permute-start = (bf16[256,512]{1,0:T(8,128)(2,1)}, bf16[256,512]{1,0:T(8,128)(2,1)S(1)}, u32[]{:S(2)}, u32[]{:S(2)}) collective-permute-start(bf16[256,512]{1,0:T(8,128)(2,1)} %param.12), channel_id=1, source_target_pairs={{0,8},{8,16},{16,24},{24,0},{1,9},{9,17},{17,25},{25,1},{2,10},{10... | collective-permute-start | bytes 786440 | tf_op jit(solution)/shard_map/ppermute | solution.py:49
  17.0 8.4 %collective-permute-start.1 = (bf16[256,512]{1,0:T(8,128)(2,1)S(1)}, bf16[256,512]{1,0:T(8,128)(2,1)S(1)}, u32[]{:S(2)}, u32[]{:S(2)}) collective-permute-start(bf16[256,512]{1,0:T(8,128)(2,1)S(1)} %collective-permute-done), channel_id=1, source_target_pairs={{0,8},{8,16},{16,24},{24,0},{1,9},{9,17},{17,25},{25,1},{2,10},{10... | collective-permute-start | bytes 786440 | tf_op jit(solution)/shard_map/ppermute | solution.py:49
  25.3 7.5 %collective-permute-start.2 = (bf16[256,512]{1,0:T(8,128)(2,1)S(1)}, bf16[256,512]{1,0:T(8,128)(2,1)S(1)}, u32[]{:S(2)}, u32[]{:S(2)}) collective-permute-start(bf16[256,512]{1,0:T(8,128)(2,1)S(1)} %collective-permute-done.1), channel_id=1, source_target_pairs={{0,8},{8,16},{16,24},{24,0},{1,9},{9,17},{17,25},{25,1},{2,10},{10... | collective-permute-start | bytes 786440 | tf_op jit(solution)/shard_map/ppermute | solution.py:49
  133.6 290.6 %reduce-scatter.5.cloned.1.call-start = ((), (), s32[]{:S(2)}) async-start(), calls=%async_computation.3 | async-start | bytes 4718592 | tf_op jit(solution)/shard_map/reduce_scatter | solution.py:60
  217.2 7.3 %collective-permute-start.3 = (bf16[256,512]{1,0:T(8,128)(2,1)S(1)}, bf16[256,512]{1,0:T(8,128)(2,1)S(1)}, u32[]{:S(2)}, u32[]{:S(2)}) collective-permute-start(bf16[256,512]{1,0:T(8,128)(2,1)S(1)} %fusion.4), channel_id=1, source_target_pairs={{0,8},{8,16},{16,24},{24,0},{1,9},{9,17},{17,25},{25,1},{2,10},{10... | collective-permute-start | bytes 786440 | tf_op jit(solution)/shard_map/ppermute | solution.py:49
  224.6 8.1 %collective-permute-start.4 = (bf16[256,512]{1,0:T(8,128)(2,1)S(1)}, bf16[256,512]{1,0:T(8,128)(2,1)S(1)}, u32[]{:S(2)}, u32[]{:S(2)}) collective-permute-start(bf16[256,512]{1,0:T(8,128)(2,1)S(1)} %collective-permute-done.3), channel_id=1, source_target_pairs={{0,8},{8,16},{16,24},{24,0},{1,9},{9,17},{17,25},{25,1},{2,10},{10... | collective-permute-start | bytes 786440 | tf_op jit(solution)/shard_map/ppermute | solution.py:49
  232.7 7.3 %collective-permute-start.5 = (bf16[256,512]{1,0:T(8,128)(2,1)S(1)}, bf16[256,512]{1,0:T(8,128)(2,1)S(1)}, u32[]{:S(2)}, u32[]{:S(2)}) collective-permute-start(bf16[256,512]{1,0:T(8,128)(2,1)S(1)} %collective-permute-done.4), channel_id=1, source_target_pairs={{0,8},{8,16},{16,24},{24,0},{1,9},{9,17},{17,25},{25,1},{2,10},{10... | collective-permute-start | bytes 786440 | tf_op jit(solution)/shard_map/ppermute | solution.py:49
  340.8 83.4 %copy-start.1 = (f32[512,512]{1,0:T(8,128)S(1)}, f32[512,512]{1,0:T(8,128)}, u32[]{:S(2)}) copy-start(f32[512,512]{1,0:T(8,128)} %param.17) | copy-start | bytes 3145732
Sparse Core Ops, SparseCore 0:
  133.7 81.3 reduce-scatter.2
  340.9 83.1 reduce-scatter.4
